TPU v7x, 32 devices: a whole 2x2x4 slice. The times are simulated.
32 devices in a mesh: groups: 2 (over x), blk: 16 (over z, y, core).
Axes of the slice: x: 2, y: 2, z: 4, core: 2. Of those that a mesh axis runs over, the one named last changes fastest.
Arguments:
- walkers: bfloat16 [64, 65536], P(('groups', 'blk')), parts along dimension 0, may hold values from -6 to 6
- intersection_inv: bfloat16 [64, 4096], P(('groups', 'blk')), parts along dimension 0, may hold values from -0.75 to 0.75
- new_slot: int32 [64], P(('groups', 'blk')), parts along dimension 0, may hold values from 0 to 31, as said below
- cholesky: bfloat16 [2048, 64, 10240], P(('groups', 'blk')), parts along dimension 0, may hold values from -0.0234375 to 0.0234375
Outputs:
- moved_walkers: bfloat16 [64, 65536], P(('groups', 'blk')), parts along dimension 0
- moved_intersection_inv: bfloat16 [64, 4096], P(('groups', 'blk')), parts along dimension 0
- force_bias: float32 [64, 10240], P(('groups', 'blk')), parts along dimension 0
There are 2 independent parts, one for each index of `groups`. A program takes and returns all parts, laid end to end along the dimension named above; each array names one. Nothing has to cross between parts.
Inputs may be any that keep to these rules, and one draw needn't show every extreme that they name: new_slot is a permutation; the new owner of walker w is new_slot[w] // 2; the 2 walkers of one device go to 2 different owners, and new_slot[w] % 2 == w % 2.
All inputs are finite; a program needn't handle non-finite values.
Results may differ from a plain program's by a relative error of at most 0.0028.
Values may be sent and summed in bfloat16 or wider, within the bound.
No kernel may reach another device: no remote copies, remote signals or barrier semaphores. Data moves between devices by JAX's collectives and lax.ppermute only.
A program may use at most 128 MiB of HBM per device.

v0:
```python
import jax
import jax.numpy as jnp
from jax import lax
from jax.sharding import PartitionSpec as P


def local(walkers, intersection_inv, new_slot, cholesky):
    cycle_size = lax.axis_size("blk")
    my_index = lax.axis_index("blk")
    walk_dev = walkers.shape[0]
    walk_total = walk_dev * cycle_size
    orbit_local = cholesky.shape[0]
    occupied = cholesky.shape[1]
    chol_flat = cholesky.reshape(orbit_local * occupied, cholesky.shape[2])
    all_slots = lax.all_gather(new_slot, "blk", axis=0, tiled=True)
    anchor = (
        jnp.zeros((walk_total,), jnp.int32)
        .at[all_slots]
        .set(jnp.arange(walk_total, dtype=jnp.int32))
    )
    local_orbit = lax.all_to_all(walkers, "blk", split_axis=1, concat_axis=0, tiled=True)
    all_inverse = lax.all_gather(intersection_inv, "blk", axis=0, tiled=True)
    perm_orbit = local_orbit[anchor]
    perm_inverse = all_inverse[anchor]
    greens = jnp.einsum(
        "wpj,wij->wpi",
        perm_orbit.reshape(walk_total, orbit_local, occupied),
        perm_inverse.reshape(walk_total, occupied, occupied),
        preferred_element_type=jnp.float32,
    ).astype(jnp.bfloat16)
    green_orbit = greens.reshape(walk_total, orbit_local * occupied)
    moved_walk = lax.all_to_all(perm_orbit, "blk", split_axis=0, concat_axis=1, tiled=True)
    moved_inverse = lax.dynamic_slice_in_dim(perm_inverse, my_index * walk_dev, walk_dev, 0)
    force_bias = lax.psum_scatter(
        jnp.dot(green_orbit, chol_flat, preferred_element_type=jnp.float32),
        "blk",
        scatter_dimension=0,
        tiled=True,
    )
    return (moved_walk, moved_inverse, force_bias)


def solution(mesh):
    placed = (
        P(("groups", "blk"), None),
        P(("groups", "blk"), None),
        P(("groups", "blk")),
        P(("groups", "blk"), None, None),
    )
    return jax.shard_map(
        local,
        mesh=mesh,
        in_specs=placed,
        out_specs=(
            P(("groups", "blk"), None),
            P(("groups", "blk"), None),
            P(("groups", "blk"), None),
        ),
        check_vma=False,
    )
```

profile of v0, /device:TPU:0, one launch (start us, length us, event | category | flops | bytes accessed | tf_op | source)
XLA Modules:
  0.0 186.7 jit_solution(3166553028669388083)
XLA Ops:
  7.2 7.4 %all-to-all-start = ((bf16[2,16,4096]{2,0,1:T(2,128)(2,1)}), bf16[2,16,4096]{2,0,1:T(2,128)(2,1)S(1)}, u32[]{:S(2)}, u32[]{:S(2)}) async-start(bf16[2,16,4096]{2,0,1:T(2,128)(2,1)} %bitcast.16), calls=%async_computation | async-start | bytes 524288 | tf_op jit(solution)/shard_map/all_to_all | solution.py:21
  14.6 0.0 all-reduce.4.cloned.1.call-start
  14.7 1.3 fusion.2
  16.6 0.9 dynamic-update-slice
  17.5 12.4 %all-reduce = s32[32]{0:T(128)S(1)} all-reduce(s32[32]{0:T(128)S(1)} %dynamic-update-slice), channel_id=1, replica_groups=mesh['groups'=2,'blk'=16] {'blk'}, use_global_device_ids=true, to_apply=%add | all-reduce | flops 32 | bytes 256
  29.9 18.9 %all-gather = bf16[16,2,4096]{2,1,0:T(2,128)(2,1)S(1)} all-gather(bf16[1,2,4096]{2,1,0:T(2,128)(2,1)} %bitcast.17), channel_id=1, replica_groups=mesh['groups'=2,'blk'=16] {'blk'}, dimensions={0}, use_global_device_ids=true | all-gather | bytes 278528 | tf_op jit(solution)/shard_map/all_gather | solution.py:22
  48.8 0.1 reshape.53
  48.9 0.7 scatter_custom_fusion
  49.6 0.7 gather_fusion.1
  50.3 0.5 reshape.21
  50.9 0.0 all-to-all-done
  50.9 0.1 all_to_all.31
  51.0 0.7 gather_fusion
  51.7 0.5 reshape.20
  52.2 0.4 fusion.3
  52.6 30.0 %convolution_bitcast_fusion = f32[32,10240]{1,0:T(8,128)} fusion(bf16[64,64,10240]{2,1,0:T(8,128)(2,1)} %param.7, bf16[32,64,64]{2,1,0:T(8,128)(2,1)S(1)} %fusion.3), kind=kOutput, calls=%fused_computation.3 | convolution fusion | flops 2684354560 | bytes 85458944 | tf_op jit(solution)/shard_map/dot_general | solution.py:35
  82.7 0.0 all-reduce.4.cloned.1.call-update
  82.7 0.9 all_to_all.32
  83.6 3.5 %all-to-all-start.1 = ((bf16[16,2,4096]{2,1,0:T(2,128)(2,1)}), bf16[16,2,4096]{2,1,0:T(2,128)(2,1)S(1)}, u32[]{:S(2)}, u32[]{:S(2)}) async-start(bf16[16,2,4096]{2,1,0:T(2,128)(2,1)} %all_to_all.32), calls=%async_computation.1 | async-start | bytes 524288 | tf_op jit(solution)/shard_map/all_to_all | solution.py:32
  87.8 0.6 constant_dynamic-slice_fusion.1
  88.4 10.8 %all-to-all-done.1 = bf16[16,2,4096]{2,1,0:T(2,128)(2,1)S(1)} async-done(((bf16[16,2,4096]{2,1,0:T(2,128)(2,1)}), bf16[16,2,4096]{2,1,0:T(2,128)(2,1)S(1)}, u32[]{:S(2)}, u32[]{:S(2)}) %all-to-all-start.1) | async-done | bytes 262176 | tf_op jit(solution)/shard_map/all_to_all | solution.py:32
  99.2 78.3 %all-reduce.4.cloned.1.call-done = f32[32,10240]{1,0:T(8,128)} async-done(((f32[32,10240]{1,0:T(8,128)}), f32[32,10240]{1,0:T(8,128)}) %all-reduce.4.cloned.1.call-update) | async-done | bytes 1310736
  177.5 1.6 constant_dynamic-slice_fusion
  179.2 0.7 copy.17
  (5 shorter events, 0.0 us)
Async XLA Ops:
  7.2 43.7 %all-to-all-start = ((bf16[2,16,4096]{2,0,1:T(2,128)(2,1)}), bf16[2,16,4096]{2,0,1:T(2,128)(2,1)S(1)}, u32[]{:S(2)}, u32[]{:S(2)}) async-start(bf16[2,16,4096]{2,0,1:T(2,128)(2,1)} %bitcast.16), calls=%async_computation | async-start | bytes 524288 | tf_op jit(solution)/shard_map/all_to_all | solution.py:21
  14.6 162.9 %all-reduce.4.cloned.1.call-start = ((), (), s32[]{:S(2)}) async-start(), calls=%async_computation.2 | async-start | bytes 2621440
  83.6 15.7 %all-to-all-start.1 = ((bf16[16,2,4096]{2,1,0:T(2,128)(2,1)}), bf16[16,2,4096]{2,1,0:T(2,128)(2,1)S(1)}, u32[]{:S(2)}, u32[]{:S(2)}) async-start(bf16[16,2,4096]{2,1,0:T(2,128)(2,1)} %all_to_all.32), calls=%async_computation.1 | async-start | bytes 524288 | tf_op jit(solution)/shard_map/all_to_all | solution.py:32
Sparse Core Ops, SparseCore 0:
  82.8 94.7 all-reduce.3
where the time goes:
time: 187 us
  waiting for transfers between devices  89.2 us (48%)
  blocking collectives  31.3 us (17%)
  matrix products  30.4 us (16%)
  between operations  15.5 us (8%)
  starting transfers between devices  11 us (6%)
  local copies, waits for them, and re-layouts  9.4 us (5%)
    unnamed x2, waiting for transfers between devices  78.3 us
    dot_general x1, matrix products, local(): jnp.dot(green_orbit, chol_flat, preferred_element_type=jnp.float32)  30 us
    all_gather x1, blocking collectives, local(): all_inverse = lax.all_gather(intersection_inv, 'blk', axis=0, tiled=True)  18.9 us
    unnamed x1, blocking collectives  12.4 us
    all_to_all x1, waiting for transfers between devices, local(): lax.all_to_all(perm_orbit, 'blk', split_axis=0, concat_axis=1, tiled=True)  10.8 us
    all_to_all x1, starting transfers between devices, local(): lax.all_to_all(walkers, 'blk', split_axis=1, concat_axis=0, tiled=True)  7.43 us
    unnamed x5, local copies, waits for them, and re-layouts  4.62 us
  transfers between devices with their start and end apart: 3, of which 2 were waited for; matrix products, arithmetic and copies ran while one was open for 3% of the time, Pallas kernels for 0%

commit v1 on v0

--- a/solution.py
+++ b/solution.py
@@ -29,7 +29,10 @@
         preferred_element_type=jnp.float32,
     ).astype(jnp.bfloat16)
     green_orbit = greens.reshape(walk_total, orbit_local * occupied)
-    moved_walk = lax.all_to_all(perm_orbit, "blk", split_axis=0, concat_axis=1, tiled=True)
+    moved_walk = jnp.concatenate(
+        lax.all_to_all(jnp.stack(jnp.split(perm_orbit, lax.axis_size("blk"), axis=0)), "blk", 0, 0),
+        axis=1,
+    )
     moved_inverse = lax.dynamic_slice_in_dim(perm_inverse, my_index * walk_dev, walk_dev, 0)
     force_bias = lax.psum_scatter(
         jnp.dot(green_orbit, chol_flat, preferred_element_type=jnp.float32),

time: 187 us -> 196 us (1.048)
  local copies, waits for them, and re-layouts: 9.4 us -> 18.5 us
    unnamed x5 -> x20, local copies, waits for them, and re-layouts: 4.62 us -> 14 us
where the time goes in v1:
time: 196 us
  waiting for transfers between devices  89.3 us (46%)
  blocking collectives  31.3 us (16%)
  matrix products  30.4 us (16%)
  local copies, waits for them, and re-layouts  18.5 us (9%)
  between operations  15.5 us (8%)
  starting transfers between devices  11 us (6%)
    unnamed x2, waiting for transfers between devices  78.5 us
    dot_general x1, matrix products, local(): jnp.dot(green_orbit, chol_flat, preferred_element_type=jnp.float32)  30 us
    all_gather x1, blocking collectives, local(): all_inverse = lax.all_gather(intersection_inv, 'blk', axis=0, tiled=True)  18.9 us
    unnamed x20, local copies, waits for them, and re-layouts  14 us
    unnamed x1, blocking collectives  12.4 us
    all_to_all x1, waiting for transfers between devices, local(): lax.all_to_all(jnp.stack(jnp.split(perm_orbit, lax.axis_size('blk'), axis...  10.8 us
    all_to_all x1, starting transfers between devices, local(): lax.all_to_all(walkers, 'blk', split_axis=1, concat_axis=0, tiled=True)  7.43 us
  transfers between devices with their start and end apart: 3, of which 2 were waited for; matrix products, arithmetic and copies ran while one was open for 3% of the time, Pallas kernels for 0%

profile of v1, /device:TPU:0, one launch (start us, length us, event | category | flops | bytes accessed | tf_op | source)
XLA Modules:
  0.0 196.0 jit_solution(2353960033464466418)
XLA Ops:
  7.2 7.4 %all-to-all-start = ((bf16[2,16,4096]{2,0,1:T(2,128)(2,1)}), bf16[2,16,4096]{2,0,1:T(2,128)(2,1)S(1)}, u32[]{:S(2)}, u32[]{:S(2)}) async-start(bf16[2,16,4096]{2,0,1:T(2,128)(2,1)} %bitcast.80), calls=%async_computation | async-start | bytes 524288 | tf_op jit(solution)/shard_map/all_to_all | solution.py:21
  14.6 0.0 all-reduce.4.cloned.1.call-start
  14.7 1.3 fusion.2
  16.6 0.9 dynamic-update-slice
  17.5 12.4 %all-reduce = s32[32]{0:T(128)S(1)} all-reduce(s32[32]{0:T(128)S(1)} %dynamic-update-slice), channel_id=1, replica_groups=mesh['groups'=2,'blk'=16] {'blk'}, use_global_device_ids=true, to_apply=%add | all-reduce | flops 32 | bytes 256
  29.9 18.9 %all-gather = bf16[16,2,4096]{2,1,0:T(2,128)(2,1)S(1)} all-gather(bf16[1,2,4096]{2,1,0:T(2,128)(2,1)} %bitcast.81), channel_id=1, replica_groups=mesh['groups'=2,'blk'=16] {'blk'}, dimensions={0}, use_global_device_ids=true | all-gather | bytes 278528 | tf_op jit(solution)/shard_map/all_gather | solution.py:22
  48.8 0.1 reshape.58
  48.9 0.7 scatter_custom_fusion
  49.6 0.7 gather_fusion.1
  50.3 0.5 reshape.26
  50.9 0.0 all-to-all-done
  50.9 0.1 all_to_all.20
  51.0 0.7 gather_fusion
  51.7 0.6 constant_dynamic-update-slice_fusion.15
  52.3 0.5 reshape.25
  52.9 0.6 constant_dynamic-update-slice_fusion.14
  53.5 0.6 constant_dynamic-update-slice_fusion.13
  54.1 0.6 constant_dynamic-update-slice_fusion.12
  54.7 0.6 constant_dynamic-update-slice_fusion.11
  55.4 0.6 constant_dynamic-update-slice_fusion.10
  56.0 0.6 constant_dynamic-update-slice_fusion.9
  56.6 0.6 constant_dynamic-update-slice_fusion.8
  57.2 0.6 constant_dynamic-update-slice_fusion.7
  57.8 0.6 constant_dynamic-update-slice_fusion.6
  58.5 0.6 constant_dynamic-update-slice_fusion.5
  59.1 0.6 constant_dynamic-update-slice_fusion.4
  59.7 0.6 constant_dynamic-update-slice_fusion.3
  60.3 0.6 constant_dynamic-update-slice_fusion.2
  61.0 0.6 constant_dynamic-update-slice_fusion.1
  61.6 0.4 fusion.3
  62.0 30.0 %convolution_bitcast_fusion = f32[32,10240]{1,0:T(8,128)} fusion(bf16[64,64,10240]{2,1,0:T(8,128)(2,1)} %param.7, bf16[32,64,64]{2,1,0:T(8,128)(2,1)S(1)} %fusion.3), kind=kOutput, calls=%fused_computation.3 | convolution fusion | flops 2684354560 | bytes 85458944 | tf_op jit(solution)/shard_map/dot_general | solution.py:38
  92.0 0.0 all-reduce.4.cloned.1.call-update
  92.0 0.6 constant_dynamic-update-slice_fusion
  92.6 3.5 %all-to-all-start.1 = ((bf16[16,2,4096]{2,1,0:T(2,128)(2,1)}), bf16[16,2,4096]{2,1,0:T(2,128)(2,1)S(1)}, u32[]{:S(2)}, u32[]{:S(2)}) async-start(bf16[16,2,4096]{2,1,0:T(2,128)(2,1)} %constant_dynamic-update-slice_fusion), calls=%async_computation.1 | async-start | bytes 524288 | tf_op jit(solution)/shard_map/all_to_all | solution.py:33
  96.8 0.6 constant_dynamic-slice_fusion.1
  97.5 10.8 %all-to-all-done.1 = bf16[16,2,4096]{2,1,0:T(2,128)(2,1)S(1)} async-done(((bf16[16,2,4096]{2,1,0:T(2,128)(2,1)}), bf16[16,2,4096]{2,1,0:T(2,128)(2,1)S(1)}, u32[]{:S(2)}, u32[]{:S(2)}) %all-to-all-start.1) | async-done | bytes 262176 | tf_op jit(solution)/shard_map/all_to_all | solution.py:33
  108.2 78.5 %all-reduce.4.cloned.1.call-done = f32[32,10240]{1,0:T(8,128)} async-done(((f32[32,10240]{1,0:T(8,128)}), f32[32,10240]{1,0:T(8,128)}) %all-reduce.4.cloned.1.call-update) | async-done | bytes 1310736
  186.8 1.6 constant_dynamic-slice_fusion
  188.4 0.7 copy.30
  (5 shorter events, 0.0 us)
Async XLA Ops:
  7.2 43.7 %all-to-all-start = ((bf16[2,16,4096]{2,0,1:T(2,128)(2,1)}), bf16[2,16,4096]{2,0,1:T(2,128)(2,1)S(1)}, u32[]{:S(2)}, u32[]{:S(2)}) async-start(bf16[2,16,4096]{2,0,1:T(2,128)(2,1)} %bitcast.80), calls=%async_computation | async-start | bytes 524288 | tf_op jit(solution)/shard_map/all_to_all | solution.py:21
  14.6 172.2 %all-reduce.4.cloned.1.call-start = ((), (), s32[]{:S(2)}) async-start(), calls=%async_computation.2 | async-start | bytes 2621440
  92.6 15.6 %all-to-all-start.1 = ((bf16[16,2,4096]{2,1,0:T(2,128)(2,1)}), bf16[16,2,4096]{2,1,0:T(2,128)(2,1)S(1)}, u32[]{:S(2)}, u32[]{:S(2)}) async-start(bf16[16,2,4096]{2,1,0:T(2,128)(2,1)} %constant_dynamic-update-slice_fusion), calls=%async_computation.1 | async-start | bytes 524288 | tf_op jit(solution)/shard_map/all_to_all | solution.py:33
Sparse Core Ops, SparseCore 0:
  92.1 94.5 all-reduce.3
